TPU v7x, 256 devices: a whole 4x4x8 slice. The times are simulated.
256 devices in a mesh: rows: 64 (over z, x, core), grp: 4 (over y).
Axes of the slice: x: 4, y: 4, z: 8, core: 2. Of those that a mesh axis runs over, the one named last changes fastest.
Arguments:
- user_features: bfloat16 [4, 16384, 256], P('grp', 'rows'), may hold values from -72 to 72
- w_first: bfloat16 [256, 256], replicated, may hold values from -0.375 to 0.375
- w_second: bfloat16 [256, 256], replicated, may hold values from -0.375 to 0.375
- item_embed: bfloat16 [4, 16384, 256], P('grp', 'rows'), may hold values from -27 to 27
- example_weight: float32 [4, 16384], P('grp', 'rows'), may hold values from 0.02 to 0.2
- positive: int32 [4, 16384], P('grp', 'rows'), may hold values from 0 to 16383
- item_owner: int32 [4, 16384, 1], P('grp', 'rows'), may hold values from 0 to 63; in each aligned block of 256 rows (0 to 255, 256 to 511, ..., all dimensions but the last counted through in order) at most 16 rows name the same one
- item_row: int32 [4, 16384], P('grp', 'rows'), may hold values from 0 to 4095
Outputs:
- grad_first: float32 [256, 256], replicated
- grad_second: float32 [256, 256], replicated
- grad_table: float32 [262144, 256], P('rows', 'grp')
Inputs may be any that keep to these rules, and one draw needn't show every extreme that they name: `item_owner`: within the rows of one device (aligned blocks of 256 pairs of a group) no owner is named by more than 16 pairs, a bound that some block reaches.
All inputs are finite; a program needn't handle non-finite values.
Results may differ from a plain program's by a relative error of at most 0.0023.
The roundings to bfloat16 on the way count: a program that leaves them out, or rounds other values in their place, can miss the bound.
Values may be sent and summed in bfloat16 or wider, within the bound.
A program may use at most 128 MiB of HBM per device.

v0:
```python
import jax
import jax.numpy as jnp
from jax import lax
from jax.sharding import Mesh
from jax.sharding import PartitionSpec as P

ITEMS_DEV = 4096
ROWS = ("rows_0", "rows_1", "rows_2")
ROWS_GRP = ("rows_0", "rows_1", "rows_2", "grp")


def gather_turned(arrays, axis, dims):
    turned = [jnp.moveaxis(a, dim, 0) for a, dim in zip(arrays, dims)]
    widths = [t[0].size for t in turned]
    both = jnp.concatenate([t.reshape(-1, w) for t, w in zip(turned, widths)], axis=1)
    filled = lax.all_gather(both, axis, axis=0, tiled=True)
    tiles = jnp.split(filled, [sum(widths[:k]) for k in range(1, len(widths))], axis=1)
    return tuple(
        (
            jnp.moveaxis(b.reshape(-1, *t.shape[1:]), 0, dim)
            for b, t, dim in zip(tiles, turned, dims)
        )
    )


def cut_along(value, dim, count):
    before, after = (value.shape[:dim], value.shape[dim + 1 :])
    return jnp.moveaxis(value.reshape(*before, count, -1, *after), dim, 0)


def sum_at_owner(value, axis, dim):
    count = lax.axis_size(axis)
    tiles = lax.all_to_all(cut_along(value, dim, count), axis, 0, 0, tiled=True)
    return jnp.sum(tiles, axis=0)


def summed_rows(value, axes, dim):
    far, near = axes
    tiles = cut_along(value, dim, lax.axis_size(far))
    nearer = sum_at_owner(tiles, near, dim + 1)
    arrived = lax.all_to_all(nearer, far, split_axis=0, concat_axis=0, tiled=True)
    return arrived.sum(axis=0)


def padded_to(lines, count):
    spare = -lines.shape[0] % count
    if not spare:
        return lines
    return jnp.concatenate([lines, jnp.zeros((spare, *lines.shape[1:]), lines.dtype)])


def sent_to_all(value, axis):
    count = lax.axis_size(axis)
    return lax.all_to_all(
        jnp.broadcast_to(value[None], (count, *value.shape)), axis, 0, 0, tiled=True
    )


def joined_along(tiles, dim):
    shape = list(tiles.shape[1:])
    shape[dim] *= tiles.shape[0]
    return jnp.moveaxis(tiles, 0, dim).reshape(shape)


def gather_axes(value, axes, dim):
    far, near = axes
    tiles = sent_to_all(sent_to_all(value, far), near)
    return joined_along(tiles.swapaxes(0, 1).reshape(-1, *value.shape), dim)


def total_of(value, axes):
    own = summed_rows(padded_to(value, lax.axis_size(axes[0]) * lax.axis_size(axes[1])), axes, 0)
    whole = gather_axes(own, axes, 0)
    return whole[: len(value)].reshape(value.shape)


def in_one(arrays, axis):
    flat, at, done = (jnp.concatenate([a.reshape(-1) for a in arrays]), 0, [])
    total = total_of(flat, axis)
    for a in arrays:
        done.append(total[at : at + a.size].reshape(a.shape))
        at += a.size
    return tuple(done)


def one_exchange(value, axis, axes, splits, concats):
    sizes = [lax.axis_size(a) for a in axes]
    tiles = cut_along(value, splits[0], sizes[0])
    tiles = jnp.moveaxis(cut_along(tiles, splits[1] + 1, sizes[1]), 0, 1)
    inside = tiles.shape[2:]
    tiles = tiles.reshape(-1, *inside)
    tiles = lax.all_to_all(tiles, axis, split_axis=0, concat_axis=0, tiled=True)
    tiles = joined_along(tiles.reshape(*sizes, *inside), concats[0] + 1)
    return joined_along(tiles, concats[1])


def contract_first(left, right):
    return lax.dot_general(
        left, right, (((0,), (0,)), ((), ())), preferred_element_type=jnp.float32
    )


def contract_last(left, right):
    return lax.dot_general(
        left, right, (((1,), (1,)), ((), ())), preferred_element_type=jnp.float32
    )


def body(
    user_features, w_first, w_second, item_embed, example_weight, positive, item_owner, item_row
):
    features = user_features[0]
    own_items = item_embed[0]
    weights = example_weight[0]
    targets = positive[0]
    owners = item_owner[0, :, 0]
    item_rows = item_row[0]
    my_users = features.shape[0]
    feature_width = own_items.shape[1]
    peers = lax.axis_size(ROWS)
    my_index = lax.axis_index(ROWS)
    pre_act = jnp.dot(features, w_first, preferred_element_type=jnp.float32)
    hidden = jax.nn.silu(pre_act).astype(jnp.bfloat16)
    user_vecs = jnp.dot(hidden, w_second, preferred_element_type=jnp.float32).astype(jnp.bfloat16)
    gathered = lax.all_gather(own_items, ROWS, axis=0, tiled=True)
    group_users = gathered.shape[0]
    scores = contract_last(user_vecs, gathered)
    row_max = jnp.max(scores, axis=1, keepdims=True)
    log_total = row_max + jnp.log(jnp.sum(jnp.exp(scores - row_max), axis=1, keepdims=True))
    columns = lax.broadcasted_iota(jnp.int32, (1, group_users), 1)
    chosen = (columns == targets[:, None]).astype(jnp.float32)
    dscore = (weights[:, None] * (jnp.exp(scores - log_total) - chosen)).astype(jnp.bfloat16)
    grad_user = jnp.dot(dscore, gathered, preferred_element_type=jnp.float32).astype(jnp.bfloat16)
    everyone = lax.all_gather(user_vecs, ROWS, axis=0, tiled=True)
    target_all, total_all, weight_all = gather_turned(
        (targets.astype(jnp.float32), log_total[:, 0], weights), ROWS, (0, 0, 0)
    )
    back_scores = contract_last(everyone, own_items)
    own_columns = my_index * my_users + lax.broadcasted_iota(jnp.int32, (1, my_users), 1)
    hits = (own_columns == target_all.astype(jnp.int32)[:, None]).astype(jnp.float32)
    back_dscore = (weight_all[:, None] * (jnp.exp(back_scores - total_all[:, None]) - hits)).astype(
        jnp.bfloat16
    )
    grad_item = contract_first(back_dscore, everyone)
    d_second = contract_first(hidden, grad_user)
    back_grad = contract_last(grad_user, w_second)
    sigmoid_pre = jax.nn.sigmoid(pre_act)
    grad_pre = (back_grad * sigmoid_pre * (1.0 + pre_act * (1.0 - sigmoid_pre))).astype(
        jnp.bfloat16
    )
    d_first = contract_first(features, grad_pre)
    grad_first, grad_second = in_one((d_first, d_second), (("rows_0", "rows_1"), ("rows_2", "grp")))
    capacity = max(2, 4 * my_users // peers)
    member = (owners[:, None] == lax.broadcasted_iota(jnp.int32, (1, peers), 1)).astype(jnp.int32)
    before = jnp.cumsum(member, axis=0) - member
    slot_rank = jnp.sum(before * member, axis=1)
    slots = owners * capacity + slot_rank
    send_grad = jnp.zeros((peers * capacity, feature_width), jnp.float32).at[slots].set(grad_item)
    send_grad = send_grad.reshape(peers, capacity, feature_width)
    send_rows = (
        jnp.full((peers * capacity,), -1.0, jnp.float32)
        .at[slots]
        .set(item_rows.astype(jnp.float32))
    )
    groups = lax.axis_size("grp")
    rows_wide = jnp.broadcast_to(send_rows.reshape(peers, capacity, 1), (peers, capacity, groups))
    got_grad, got_rows = (
        one_exchange(send_grad, ROWS_GRP, (ROWS, "grp"), (0, 2), (0, 1)),
        one_exchange(rows_wide, ROWS_GRP, (ROWS, "grp"), (0, 2), (0, 1)),
    )
    share_width = feature_width // groups
    table_rows = got_rows.reshape(-1).astype(jnp.int32)
    table_rows = jnp.where(table_rows >= 0, table_rows, ITEMS_DEV)
    grad_table = (
        jnp.zeros((ITEMS_DEV, share_width), jnp.float32)
        .at[table_rows]
        .add(got_grad.reshape(-1, share_width), mode="drop")
    )
    return (grad_first, grad_second, grad_table)


def solution(mesh):
    torus = Mesh(
        mesh.devices.reshape(8, 4, 2, mesh.shape["grp"]), ("rows_0", "rows_1", "rows_2", "grp")
    )
    placed = (
        P("grp", ROWS, None),
        P(),
        P(),
        P("grp", ROWS, None),
        P("grp", ROWS),
        P("grp", ROWS),
        P("grp", ROWS, None),
        P("grp", ROWS),
    )
    return jax.shard_map(
        body, mesh=torus, in_specs=placed, out_specs=(P(), P(), P(ROWS, "grp")), check_vma=False
    )
```

profile of v0, /device:TPU:1, one launch (start us, length us, event | category | flops | bytes accessed | tf_op | source)
XLA Modules:
  0.0 337.8 jit_solution(12011691266853101209)
XLA Ops:
  7.2 0.0 copy-start
  7.2 0.0 all-gather.6.cloned.1.call-start
  7.2 0.7 all-gather.6.cloned.1.call-update
  7.9 0.0 all-gather.4.cloned.1.call-start
  8.0 1.1 fusion.24
  9.1 0.9 convolution_convert_fusion
  10.0 0.0 all-gather.4.cloned.1.call-update
  10.0 0.7 fusion.30
  10.7 0.6 reduce-window.6
  11.3 0.2 slice_reduce_fusion
  11.5 0.7 convert_element_type.84
  12.2 0.8 fusion.29
  13.0 84.9 %all-gather.6.cloned.1.call-done = bf16[1,16384,256]{2,1,0:T(8,128)(2,1)} async-done(((bf16[1,256,256]{2,1,0:T(8,128)(2,1)}), bf16[1,16384,256]{2,1,0:T(8,128)(2,1)}) %all-gather.6.cloned.1.call-update) | async-done | bytes 8388624 | tf_op jit(solution)/shard_map/all_gather | solution.py:125
  97.9 11.6 %fusion.36 = (f32[256]{0:T(256)S(1)}, f32[256,16384]{1,0:T(8,128)}) fusion(bf16[256,256]{1,0:T(8,128)(2,1)} %convolution_convert_fusion, bf16[1,16384,256]{2,1,0:T(8,128)(2,1)} %all-gather.6.cloned.1.call-done), kind=kOutput, calls=%fused_computation.61 | convolution fusion | flops 2151677696 | bytes 25297920 | tf_op jit(solution)/shard_map/dot_general | solution.py:104
  109.5 8.3 %exponential_reduce_fusion = f32[256]{0:T(256)S(1)} fusion(f32[256,16384]{1,0:T(8,128)} %get-tuple-element.21, f32[256]{0:T(256)S(1)} %get-tuple-element.20), kind=kLoop, calls=%fused_computation.10 | loop fusion | flops 8388352 | bytes 16779264 | tf_op jit(solution)/shard_map/reduce_sum | solution.py:129
  117.8 0.0 copy-start.2
  117.8 0.0 copy-start.3
  117.8 13.0 %fusion.11 = bf16[256,256]{1,0:T(8,128)(2,1)S(1)} fusion(bf16[1,16384,256]{2,1,0:T(8,128)(2,1)} %all-gather.6.cloned.1.call-done, f32[256,16384]{1,0:T(8,128)} %get-tuple-element.21, s32[256]{0:T(256)S(1)} %bitcast.120, f32[256]{0:T(256)S(1)} %log_add_fusion, f32[256]{0:T(256)S(1)} %bitcast.116), kind=kOutput, calls=%fused_computation.21 | convolution fusion | flops 2172715008 | bytes 25299968 | tf_op jit(solution)/shard_map/dot_general | solution.py:133
  130.9 0.0 copy-start.1
  130.9 0.3 fusion.34
  131.1 0.1 concatenate.12
  131.2 0.5 convolution_bitcast_fusion
  131.7 0.1 copy.24
  131.8 0.1 concatenate.11
  132.0 1.1 copy.25
  133.1 4.5 %all-to-all-start = ((f32[8,32,512]{2,1,0:T(8,128)}), f32[8,32,512]{2,1,0:T(8,128)S(1)}, u32[]{:S(2)}, u32[]{:S(2)}) async-start(f32[8,32,512]{2,1,0:T(8,128)} %copy.25), calls=%async_computation | async-start | bytes 1048576 | tf_op jit(solution)/shard_map/all_to_all | solution.py:33
  137.6 1.4 scatter_custom_fusion
  139.0 0.1 broadcast_in_dim.43
  139.1 7.8 %all-to-all-done = f32[8,32,512]{2,1,0:T(8,128)S(1)} async-done(((f32[8,32,512]{2,1,0:T(8,128)}), f32[8,32,512]{2,1,0:T(8,128)S(1)}, u32[]{:S(2)}, u32[]{:S(2)}) %all-to-all-start) | async-done | bytes 524320 | tf_op jit(solution)/shard_map/all_to_all | solution.py:33
  147.0 0.7 all_to_all.23
  147.7 5.1 %all-to-all-start.1 = ((f32[32,1,512]{2,1,0:T(1,128)}), f32[32,1,512]{2,1,0:T(1,128)S(1)}, u32[]{:S(2)}, u32[]{:S(2)}) async-start(f32[32,1,512]{2,1,0:T(1,128)} %all_to_all.23), calls=%async_computation.1 | async-start | bytes 131072 | tf_op jit(solution)/shard_map/all_to_all | solution.py:41
  152.8 45.7 %all_gather.10 = f32[16384,3]{0,1:T(4,128)S(1)} all-gather(f32[256,3]{0,1:T(4,128)S(1)} %pad_maximum_fusion), channel_id=1, replica_groups=mesh['rows_0'=8,'rows_1'=4,'rows_2'=2,'grp'=4] {'rows_0','rows_1','rows_2'}, dimensions={0}, use_global_device_ids=true | all-gather | bytes 199680 | tf_op jit(solution)/shard_map/all_gather | solution.py:16
  198.5 0.0 all-to-all-done.1
  198.5 0.1 reduce_sum.40
  198.6 0.7 broadcast_in_dim.17
  199.2 6.6 %all-to-all-start.2 = ((f32[32,1,512]{2,1,0:T(1,128)}), f32[32,1,512]{2,1,0:T(1,128)S(1)}, u32[]{:S(2)}, u32[]{:S(2)}) async-start(f32[32,1,512]{2,1,0:T(1,128)} %broadcast_in_dim.17), calls=%async_computation.2 | async-start | bytes 131072 | tf_op jit(solution)/shard_map/all_to_all | solution.py:54
  205.8 0.1 slice_convert_fusion
  206.0 8.7 %all-to-all-done.2 = f32[32,1,512]{2,1,0:T(1,128)S(1)} async-done(((f32[32,1,512]{2,1,0:T(1,128)}), f32[32,1,512]{2,1,0:T(1,128)S(1)}, u32[]{:S(2)}, u32[]{:S(2)}) %all-to-all-start.2) | async-done | bytes 65568 | tf_op jit(solution)/shard_map/all_to_all | solution.py:54
  214.7 0.7 transpose_transpose.8
  215.4 6.6 %all-to-all-start.4 = ((f32[256,1,16,1]{2,3,1,0:T(1,128)}), f32[256,1,16,1]{2,3,1,0:T(1,128)S(1)}, u32[]{:S(2)}, u32[]{:S(2)}) async-start(f32[256,1,16,1]{2,3,1,0:T(1,128)} %bitcast.14), calls=%async_computation.4 | async-start | bytes 262144 | tf_op jit(solution)/shard_map/all_to_all | solution.py:92
  222.0 0.0 all-gather.4.cloned.1.call-done
  222.0 12.5 %fusion.3.clone.4 = bf16[16384,256]{1,0:T(8,128)(2,1)} fusion(bf16[16384,256]{1,0:T(8,128)(2,1)} %all-gather.4.cloned.1.call-done, s32[256]{0:T(256)S(1)} %iota_add_fusion, f32[16384]{0:T(1024)S(1)} %bitcast.109, f32[16384]{0:T(1024)S(1)} %bitcast.110, s32[16384]{0:T(1024)S(1)} %bitcast.108, bf16[1,256,256]{2,1,0:T(8,128)(2,1)S(1)} %copy-done.1), kind=kOutput, calls=%fused_computation.7.clone.clone.clone.1 | convolution fusion | flops 2172649472 | bytes 17105920 | tf_op jit(solution)/shard_map/dot_general | solution.py:104
  234.5 0.2 all-to-all-done.4
  234.8 0.9 broadcast_in_dim.19
  235.7 6.1 %all-to-all-start.3 = ((f32[8,32,512]{2,1,0:T(8,128)}), f32[8,32,512]{2,1,0:T(8,128)}, u32[]{:S(2)}, u32[]{:S(2)}) async-start(f32[8,32,512]{2,1,0:T(8,128)} %broadcast_in_dim.19), calls=%async_computation.3 | async-start | bytes 1048576 | tf_op jit(solution)/shard_map/all_to_all | solution.py:54
  241.8 8.1 %fusion.8 = f32[256,256]{1,0:T(8,128)S(1)} fusion(bf16[16384,256]{1,0:T(8,128)(2,1)} %all-gather.4.cloned.1.call-done, bf16[16384,256]{1,0:T(8,128)(2,1)} %fusion.3.clone.4), kind=kOutput, calls=%fused_computation.15 | convolution fusion | flops 2147483648 | bytes 17039360 | tf_op jit(solution)/shard_map/dot_general | solution.py:98
  249.9 1.7 scatter_custom_fusion.1
  251.6 0.9 reshape_reshape_reshape.3
  252.5 1.5 copy.29
  254.0 3.4 %reshape.203 = f32[256,1,1024]{2,1,0:T(1,128)} reshape(f32[256,1,16,64]{3,2,1,0:T(8,128)} %bitcast.104) | data formatting | bytes 2097152
  257.5 12.3 %all-to-all-start.5 = ((f32[256,1,1024]{2,1,0:T(1,128)}), f32[256,1,1024]{2,1,0:T(1,128)S(1)}, u32[]{:S(2)}, u32[]{:S(2)}) async-start(f32[256,1,1024]{2,1,0:T(1,128)} %reshape.203), calls=%async_computation.5 | async-start | bytes 2097152 | tf_op jit(solution)/shard_map/all_to_all | solution.py:92
  269.8 0.1 convert_element_type.96
  269.9 0.1 convert_element_type.90
  270.1 1.1 fusion.35
  271.2 0.2 copy.26
  271.3 0.7 reshape.163
  272.1 0.2 copy.27
  272.2 0.7 reshape.164
  273.0 27.7 %all-to-all-done.5 = f32[256,1,1024]{2,1,0:T(1,128)S(1)} async-done(((f32[256,1,1024]{2,1,0:T(1,128)}), f32[256,1,1024]{2,1,0:T(1,128)S(1)}, u32[]{:S(2)}, u32[]{:S(2)}) %all-to-all-start.5) | async-done | bytes 1048608 | tf_op jit(solution)/shard_map/all_to_all | solution.py:92
  300.6 0.5 broadcast.102
  301.2 3.1 reduce.3
  304.3 1.9 reshape.204
  306.2 23.2 %scatter_custom_fusion.2 = f32[4096,64]{1,0:T(8,128)S(1)} fusion(s32[4096]{0:T(1024)S(1)} %bitcast.111, f32[4096,64]{1,0:T(8,128)} %bitcast.105, f32[]{:T(128)} %constant.18.clone.1), kind=kCustom, calls=%fused_computation.22 | custom fusion | flops 262144 | bytes 1049088 | tf_op jit(solution)/shard_map/scatter-add | solution.py:177
  329.4 1.6 copy.31
  (20 shorter events, 0.2 us)
Async XLA Ops:
  7.2 2.0 copy-start
  7.2 90.7 %all-gather.6.cloned.1.call-start = ((), (), s32[]{:S(2)}) async-start(), calls=%async_computation.7 | async-start | bytes 8519680 | tf_op jit(solution)/shard_map/all_gather | solution.py:125
  7.9 214.1 %all-gather.4.cloned.1.call-start = ((), (), s32[]{:S(2)}) async-start(), calls=%async_computation.6 | async-start | bytes 8519680 | tf_op jit(solution)/shard_map/all_gather | solution.py:134
  109.5 8.3 %copy-start.4 = (f32[1,256]{1,0:T(1,128)S(1)}, f32[1,256]{1,0:T(1,128)}, u32[]{:S(2)}) copy-start(f32[1,256]{1,0:T(1,128)} %param.12) | copy-start | bytes 3076
  109.5 8.3 %copy-start.5 = (s32[1,256]{1,0:T(1,128)S(1)}, s32[1,256]{1,0:T(1,128)}, u32[]{:S(2)}) copy-start(s32[1,256]{1,0:T(1,128)} %param.13) | copy-start | bytes 3076
  117.8 13.4 %copy-start.2 = (bf16[1,256,256]{2,1,0:T(8,128)(2,1)S(1)}, bf16[1,256,256]{2,1,0:T(8,128)(2,1)}, u32[]{:S(2)}) copy-start(bf16[1,256,256]{2,1,0:T(8,128)(2,1)} %param.8) | copy-start | bytes 393220
  117.8 19.8 %copy-start.3 = (s32[1,256,1]{1,2,0:T(1,128)S(1)}, s32[1,256,1]{1,2,0:T(1,128)}, u32[]{:S(2)}) copy-start(s32[1,256,1]{1,2,0:T(1,128)} %param.14) | copy-start | bytes 3076
  130.9 91.1 %copy-start.1 = (bf16[1,256,256]{2,1,0:T(8,128)(2,1)S(1)}, bf16[1,256,256]{2,1,0:T(8,128)(2,1)}, u32[]{:S(2)}) copy-start(bf16[1,256,256]{2,1,0:T(8,128)(2,1)} %param.11) | copy-start | bytes 393220
  133.1 13.9 %all-to-all-start = ((f32[8,32,512]{2,1,0:T(8,128)}), f32[8,32,512]{2,1,0:T(8,128)S(1)}, u32[]{:S(2)}, u32[]{:S(2)}) async-start(f32[8,32,512]{2,1,0:T(8,128)} %copy.25), calls=%async_computation | async-start | bytes 1048576 | tf_op jit(solution)/shard_map/all_to_all | solution.py:33
  147.7 50.8 %all-to-all-start.1 = ((f32[32,1,512]{2,1,0:T(1,128)}), f32[32,1,512]{2,1,0:T(1,128)S(1)}, u32[]{:S(2)}, u32[]{:S(2)}) async-start(f32[32,1,512]{2,1,0:T(1,128)} %all_to_all.23), calls=%async_computation.1 | async-start | bytes 131072 | tf_op jit(solution)/shard_map/all_to_all | solution.py:41
  199.2 15.5 %all-to-all-start.2 = ((f32[32,1,512]{2,1,0:T(1,128)}), f32[32,1,512]{2,1,0:T(1,128)S(1)}, u32[]{:S(2)}, u32[]{:S(2)}) async-start(f32[32,1,512]{2,1,0:T(1,128)} %broadcast_in_dim.17), calls=%async_computation.2 | async-start | bytes 131072 | tf_op jit(solution)/shard_map/all_to_all | solution.py:54
  215.4 19.4 %all-to-all-start.4 = ((f32[256,1,16,1]{2,3,1,0:T(1,128)}), f32[256,1,16,1]{2,3,1,0:T(1,128)S(1)}, u32[]{:S(2)}, u32[]{:S(2)}) async-start(f32[256,1,16,1]{2,3,1,0:T(1,128)} %bitcast.14), calls=%async_computation.4 | async-start | bytes 262144 | tf_op jit(solution)/shard_map/all_to_all | solution.py:92
  235.7 21.8 %all-to-all-start.3 = ((f32[8,32,512]{2,1,0:T(8,128)}), f32[8,32,512]{2,1,0:T(8,128)}, u32[]{:S(2)}, u32[]{:S(2)}) async-start(f32[8,32,512]{2,1,0:T(8,128)} %broadcast_in_dim.19), calls=%async_computation.3 | async-start | bytes 1048576 | tf_op jit(solution)/shard_map/all_to_all | solution.py:54
  257.5 43.2 %all-to-all-start.5 = ((f32[256,1,1024]{2,1,0:T(1,128)}), f32[256,1,1024]{2,1,0:T(1,128)S(1)}, u32[]{:S(2)}, u32[]{:S(2)}) async-start(f32[256,1,1024]{2,1,0:T(1,128)} %reshape.203), calls=%async_computation.5 | async-start | bytes 2097152 | tf_op jit(solution)/shard_map/all_to_all | solution.py:92
Sparse Core Ops, SparseCore 0:
  10.8 87.1 all-gather.5
  101.3 79.9 all-gather.3
where the time goes:
time: 338 us
  waiting for transfers between devices  130 us (38%)
  matrix products  48 us (14%)
  blocking collectives  45.7 us (14%)
  starting transfers between devices  41.3 us (12%)
  other arithmetic  37.8 us (11%)
  local copies, waits for them, and re-layouts  20.6 us (6%)
  between operations  14.3 us (4%)
    all_gather x1, waiting for transfers between devices, body(): gathered = lax.all_gather(own_items, ROWS, axis=0, tiled=True)  84.9 us
    all_gather x1, blocking collectives, gather_turned(): filled = lax.all_gather(both, axis, axis=0, tiled=True)  45.7 us
    all_to_all x2, waiting for transfers between devices, one_exchange(): tiles = lax.all_to_all(tiles, axis, split_axis=0, concat_axis=0, tiled=True)  27.9 us
    dot_general x2, matrix products, contract_last(): lax.dot_general(left, right, (((1,), (1,)), ((), ())), preferred_element_...  24.1 us
    scatter-add x1, other arithmetic, body(): grad_table = jnp.zeros((ITEMS_DEV, share_width), jnp.float32).at[table_ro...  23.2 us
    all_to_all x2, starting transfers between devices, one_exchange(): tiles = lax.all_to_all(tiles, axis, split_axis=0, concat_axis=0, tiled=True)  18.9 us
    dot_general x1, matrix products, body(): jnp.dot(dscore, gathered, preferred_element_type=jnp.float32)  13 us
    all_to_all x2, starting transfers between devices, sent_to_all(): lax.all_to_all(jnp.broadcast_to(value[None], (count, *value.shape)), axis...  12.7 us
  transfers between devices with their start and end apart: 8, of which 5 were waited for; matrix products, arithmetic and copies ran while one was open for 22% of the time, Pallas kernels for 0%

commit v1 on v0

--- a/solution.py
+++ b/solution.py
@@ -7,6 +7,11 @@
 ITEMS_DEV = 4096
 ROWS = ("rows_0", "rows_1", "rows_2")
 ROWS_GRP = ("rows_0", "rows_1", "rows_2", "grp")
+
+
+def swapped_in(block, name, along):
+    outgoing = jnp.stack([block] * lax.axis_size(name))
+    return jnp.concatenate(lax.all_to_all(outgoing, name, 0, 0), axis=along)
 
 
 def gather_turned(arrays, axis, dims):
@@ -122,7 +127,7 @@
     pre_act = jnp.dot(features, w_first, preferred_element_type=jnp.float32)
     hidden = jax.nn.silu(pre_act).astype(jnp.bfloat16)
     user_vecs = jnp.dot(hidden, w_second, preferred_element_type=jnp.float32).astype(jnp.bfloat16)
-    gathered = lax.all_gather(own_items, ROWS, axis=0, tiled=True)
+    gathered = swapped_in(own_items, ROWS, 0)
     group_users = gathered.shape[0]
     scores = contract_last(user_vecs, gathered)
     row_max = jnp.max(scores, axis=1, keepdims=True)

time: 338 us -> 477 us (1.41)
  waiting for transfers between devices: 130 us -> 249 us
  starting transfers between devices: 41.3 us -> 59 us
  local copies, waits for them, and re-layouts: 20.6 us -> 25.8 us
    all_to_all x0 -> x1, waiting for transfers between devices: none -> 205 us  [swapped_in(): return jnp.concatenate(lax.all_to_all(outgoing, name, 0, 0), axis=along)]
    all_gather x1 -> x0, waiting for transfers between devices: 84.9 us -> none  [body(): gathered = lax.all_gather(own_items, ROWS, axis=0, tiled=True)]
    all_to_all x0 -> x1, starting transfers between devices: none -> 13.3 us  [swapped_in(): return jnp.concatenate(lax.all_to_all(outgoing, name, 0, 0), axis=along)]
    another operation x1 -> x2, local copies, waits for them, and re-layouts: 0.01 us -> 5.18 us  [the longest x1 5.17 us: swapped_in(): outgoing = jnp.stack([block] * lax.axis_size(name))]
  transfers between devices with their start and end apart: 8 -> 8, of which waited for: 5 -> 5; matrix products, arithmetic and copies ran while one was open for 22% -> 15% of each run, Pallas kernels for 0% -> 0%
where the time goes in v1:
time: 477 us; the launch traced here: 476 us
  waiting for transfers between devices  249 us (52%)
  starting transfers between devices  59 us (12%)
  matrix products  46.9 us (10%)
  blocking collectives  45.4 us (10%)
  other arithmetic  35.6 us (7%)
  local copies, waits for them, and re-layouts  25.8 us (5%)
  between operations  14.4 us (3%)
    all_to_all x1, waiting for transfers between devices, swapped_in(): return jnp.concatenate(lax.all_to_all(outgoing, name, 0, 0), axis=along)  205 us
    all_gather x1, blocking collectives, gather_turned(): filled = lax.all_gather(both, axis, axis=0, tiled=True)  45.4 us
    all_to_all x2, waiting for transfers between devices, one_exchange(): tiles = lax.all_to_all(tiles, axis, split_axis=0, concat_axis=0, tiled=True)  27.9 us
    dot_general x2, matrix products, contract_last(): lax.dot_general(left, right, (((1,), (1,)), ((), ())), preferred_element_...  24.1 us
    scatter-add x1, other arithmetic, body(): grad_table = jnp.zeros((ITEMS_DEV, share_width), jnp.float32).at[table_ro...  23.2 us
    all_to_all x2, starting transfers between devices, one_exchange(): tiles = lax.all_to_all(tiles, axis, split_axis=0, concat_axis=0, tiled=True)  18.9 us
    all_to_all x1, starting transfers between devices, swapped_in(): return jnp.concatenate(lax.all_to_all(outgoing, name, 0, 0), axis=along)  13.3 us
    dot_general x1, matrix products, body(): jnp.dot(dscore, gathered, preferred_element_type=jnp.float32)  12.9 us
  transfers between devices with their start and end apart: 8, of which 5 were waited for; matrix products, arithmetic and copies ran while one was open for 15% of the time, Pallas kernels for 0%

profile of v1, /device:TPU:1, one launch (start us, length us, event | category | flops | bytes accessed | tf_op | source)
XLA Modules:
  0.0 476.4 jit_solution(4701458576502261874)
XLA Ops:
  7.2 0.0 copy-start
  7.2 5.2 %stack.3 = bf16[64,256,256]{2,1,0:T(8,128)(2,1)} broadcast(bf16[256,256]{1,0:T(8,128)(2,1)} %bitcast.102), dimensions={1,2} | broadcast | bytes 8519680 | tf_op jit(solution)/shard_map/stack | solution.py:13
  12.4 13.3 %all-to-all-start = ((bf16[64,256,256]{2,1,0:T(8,128)(2,1)}), bf16[64,256,256]{2,1,0:T(8,128)(2,1)}, u32[]{:S(2)}, u32[]{:S(2)}) async-start(bf16[64,256,256]{2,1,0:T(8,128)(2,1)} %stack.3), calls=%async_computation | async-start | bytes 16777216 | tf_op jit(solution)/shard_map/all_to_all | solution.py:14
  25.7 0.0 all-gather.2.cloned.1.call-start
  25.7 0.0 copy-done.3
  25.7 0.0 copy-done.4
  25.7 0.2 fusion.17
  25.9 0.0 copy-done
  25.9 0.9 convolution_convert_fusion
  26.8 0.0 all-gather.2.cloned.1.call-update
  26.9 0.6 reduce-window.6
  27.5 0.2 slice_reduce_fusion
  27.7 0.1 fusion.22
  27.8 204.8 %all-to-all-done = bf16[64,256,256]{2,1,0:T(8,128)(2,1)} async-done(((bf16[64,256,256]{2,1,0:T(8,128)(2,1)}), bf16[64,256,256]{2,1,0:T(8,128)(2,1)}, u32[]{:S(2)}, u32[]{:S(2)}) %all-to-all-start) | async-done | bytes 8388640 | tf_op jit(solution)/shard_map/all_to_all | solution.py:14
  232.7 11.6 %fusion.31 = (f32[256]{0:T(256)S(1)}, f32[256,16384]{1,0:T(8,128)}) fusion(bf16[256,256]{1,0:T(8,128)(2,1)} %convolution_convert_fusion, bf16[16384,256]{1,0:T(8,128)(2,1)} %bitcast.3), kind=kOutput, calls=%fused_computation.58 | convolution fusion | flops 2151677696 | bytes 25297920 | tf_op jit(solution)/shard_map/dot_general | solution.py:109
  244.2 8.2 %exponential_reduce_fusion = f32[256]{0:T(256)S(1)} fusion(f32[256,16384]{1,0:T(8,128)} %get-tuple-element.21, f32[256]{0:T(256)S(1)} %get-tuple-element.20), kind=kLoop, calls=%fused_computation.10 | loop fusion | flops 8388352 | bytes 16779264 | tf_op jit(solution)/shard_map/reduce_sum | solution.py:134
  252.4 12.9 %fusion.8 = bf16[256,256]{1,0:T(8,128)(2,1)S(1)} fusion(bf16[16384,256]{1,0:T(8,128)(2,1)} %bitcast.3, f32[256,16384]{1,0:T(8,128)} %get-tuple-element.21, s32[256]{0:T(256)S(1)} %bitcast.115, f32[256]{0:T(256)S(1)} %log_add_fusion, f32[256]{0:T(256)S(1)} %bitcast.111), kind=kOutput, calls=%fused_computation.18 | convolution fusion | flops 2172715008 | bytes 25299968 | tf_op jit(solution)/shard_map/dot_general | solution.py:138
  265.3 0.0 copy-start.2
  265.4 0.3 fusion.29
  265.6 0.1 concatenate.12
  265.7 0.5 convolution_bitcast_fusion
  266.2 0.1 copy.24
  266.3 0.1 concatenate.11
  266.4 1.1 copy.25
  267.6 8.6 %all-to-all-start.1 = ((f32[8,32,512]{2,1,0:T(8,128)}), f32[8,32,512]{2,1,0:T(8,128)S(1)}, u32[]{:S(2)}, u32[]{:S(2)}) async-start(f32[8,32,512]{2,1,0:T(8,128)} %copy.25), calls=%async_computation.1 | async-start | bytes 1048576 | tf_op jit(solution)/shard_map/all_to_all | solution.py:38
  276.1 1.4 scatter_custom_fusion
  277.6 0.1 broadcast_in_dim.43
  277.6 7.8 %all-to-all-done.1 = f32[8,32,512]{2,1,0:T(8,128)S(1)} async-done(((f32[8,32,512]{2,1,0:T(8,128)}), f32[8,32,512]{2,1,0:T(8,128)S(1)}, u32[]{:S(2)}, u32[]{:S(2)}) %all-to-all-start.1) | async-done | bytes 524320 | tf_op jit(solution)/shard_map/all_to_all | solution.py:38
  285.5 0.7 all_to_all.27
  286.2 5.4 %all-to-all-start.2 = ((f32[32,1,512]{2,1,0:T(1,128)}), f32[32,1,512]{2,1,0:T(1,128)S(1)}, u32[]{:S(2)}, u32[]{:S(2)}) async-start(f32[32,1,512]{2,1,0:T(1,128)} %all_to_all.27), calls=%async_computation.2 | async-start | bytes 131072 | tf_op jit(solution)/shard_map/all_to_all | solution.py:46
  291.6 45.4 %all_gather.6 = f32[16384,3]{0,1:T(4,128)S(1)} all-gather(f32[256,3]{0,1:T(4,128)S(1)} %pad_maximum_fusion), channel_id=1, replica_groups=mesh['rows_0'=8,'rows_1'=4,'rows_2'=2,'grp'=4] {'rows_0','rows_1','rows_2'}, dimensions={0}, use_global_device_ids=true | all-gather | bytes 199680 | tf_op jit(solution)/shard_map/all_gather | solution.py:21
  337.0 0.0 all-to-all-done.2
  337.0 0.1 reduce_sum.40
  337.1 0.7 broadcast_in_dim.17
  337.7 6.7 %all-to-all-start.3 = ((f32[32,1,512]{2,1,0:T(1,128)}), f32[32,1,512]{2,1,0:T(1,128)S(1)}, u32[]{:S(2)}, u32[]{:S(2)}) async-start(f32[32,1,512]{2,1,0:T(1,128)} %broadcast_in_dim.17), calls=%async_computation.3 | async-start | bytes 131072 | tf_op jit(solution)/shard_map/all_to_all | solution.py:59
  344.4 0.1 slice_convert_fusion
  344.6 8.7 %all-to-all-done.3 = f32[32,1,512]{2,1,0:T(1,128)S(1)} async-done(((f32[32,1,512]{2,1,0:T(1,128)}), f32[32,1,512]{2,1,0:T(1,128)S(1)}, u32[]{:S(2)}, u32[]{:S(2)}) %all-to-all-start.3) | async-done | bytes 65568 | tf_op jit(solution)/shard_map/all_to_all | solution.py:59
  353.3 0.7 transpose_transpose.8
  354.0 6.6 %all-to-all-start.5 = ((f32[256,1,16,1]{2,3,1,0:T(1,128)}), f32[256,1,16,1]{2,3,1,0:T(1,128)S(1)}, u32[]{:S(2)}, u32[]{:S(2)}) async-start(f32[256,1,16,1]{2,3,1,0:T(1,128)} %bitcast.15), calls=%async_computation.5 | async-start | bytes 262144 | tf_op jit(solution)/shard_map/all_to_all | solution.py:97
  360.5 0.0 all-gather.2.cloned.1.call-done
  360.6 12.5 %fusion.3.clone.4 = bf16[16384,256]{1,0:T(8,128)(2,1)} fusion(bf16[16384,256]{1,0:T(8,128)(2,1)} %all-gather.2.cloned.1.call-done, s32[256]{0:T(256)S(1)} %iota_add_fusion, f32[16384]{0:T(1024)S(1)} %bitcast.104, f32[16384]{0:T(1024)S(1)} %bitcast.105, s32[16384]{0:T(1024)S(1)} %bitcast.103, bf16[1,256,256]{2,1,0:T(8,128)(2,1)S(1)} %copy-done.2), kind=kOutput, calls=%fused_computation.7.clone.clone.clone.1 | convolution fusion | flops 2172649472 | bytes 17105920 | tf_op jit(solution)/shard_map/dot_general | solution.py:109
  373.1 0.2 all-to-all-done.5
  373.4 0.9 broadcast_in_dim.19
  374.3 6.1 %all-to-all-start.4 = ((f32[8,32,512]{2,1,0:T(8,128)}), f32[8,32,512]{2,1,0:T(8,128)}, u32[]{:S(2)}, u32[]{:S(2)}) async-start(f32[8,32,512]{2,1,0:T(8,128)} %broadcast_in_dim.19), calls=%async_computation.4 | async-start | bytes 1048576 | tf_op jit(solution)/shard_map/all_to_all | solution.py:59
  380.4 8.1 %fusion.5 = f32[256,256]{1,0:T(8,128)S(1)} fusion(bf16[16384,256]{1,0:T(8,128)(2,1)} %all-gather.2.cloned.1.call-done, bf16[16384,256]{1,0:T(8,128)(2,1)} %fusion.3.clone.4), kind=kOutput, calls=%fused_computation.12 | convolution fusion | flops 2147483648 | bytes 17039360 | tf_op jit(solution)/shard_map/dot_general | solution.py:103
  388.5 1.7 scatter_custom_fusion.1
  390.2 0.9 reshape_reshape_reshape.3
  391.1 1.5 copy.29
  392.6 3.5 reshape.207
  396.1 0.0 all-to-all-done.4
  396.1 12.3 %all-to-all-start.6 = ((f32[256,1,1024]{2,1,0:T(1,128)}), f32[256,1,1024]{2,1,0:T(1,128)S(1)}, u32[]{:S(2)}, u32[]{:S(2)}) async-start(f32[256,1,1024]{2,1,0:T(1,128)} %reshape.207), calls=%async_computation.6 | async-start | bytes 2097152 | tf_op jit(solution)/shard_map/all_to_all | solution.py:97
  408.4 0.1 convert_element_type.96
  408.5 0.1 convert_element_type.90
  408.7 1.1 fusion.30
  409.8 0.2 copy.26
  409.9 0.7 reshape.168
  410.7 0.2 copy.27
  410.8 0.7 reshape.169
  411.6 27.7 %all-to-all-done.6 = f32[256,1,1024]{2,1,0:T(1,128)S(1)} async-done(((f32[256,1,1024]{2,1,0:T(1,128)}), f32[256,1,1024]{2,1,0:T(1,128)S(1)}, u32[]{:S(2)}, u32[]{:S(2)}) %all-to-all-start.6) | async-done | bytes 1048608 | tf_op jit(solution)/shard_map/all_to_all | solution.py:97
  439.3 0.5 broadcast.103
  439.8 3.1 reduce.3
  442.9 1.9 reshape.208
  444.8 23.2 %scatter_custom_fusion.2 = f32[4096,64]{1,0:T(8,128)S(1)} fusion(s32[4096]{0:T(1024)S(1)} %bitcast.106, f32[4096,64]{1,0:T(8,128)} %bitcast.99, f32[]{:T(128)} %constant.18.clone.1), kind=kCustom, calls=%fused_computation.19 | custom fusion | flops 262144 | bytes 1049088 | tf_op jit(solution)/shard_map/scatter-add | solution.py:182
  468.0 1.6 copy.31
  (26 shorter events, 0.2 us)
Async XLA Ops:
  7.2 18.8 %copy-start = (bf16[256,256]{1,0:T(8,128)(2,1)S(1)}, bf16[256,256]{1,0:T(8,128)(2,1)}, u32[]{:S(2)}) copy-start(bf16[256,256]{1,0:T(8,128)(2,1)} %param.10) | copy-start | bytes 393220
  12.4 13.4 %copy-start.3 = (bf16[256,256]{1,0:T(8,128)(2,1)S(1)}, bf16[256,256]{1,0:T(8,128)(2,1)}, u32[]{:S(2)}) copy-start(bf16[256,256]{1,0:T(8,128)(2,1)} %param.9) | copy-start | bytes 393220
  12.4 13.4 %copy-start.4 = (bf16[1,256,256]{2,1,0:T(8,128)(2,1)S(1)}, bf16[1,256,256]{2,1,0:T(8,128)(2,1)}, u32[]{:S(2)}) copy-start(bf16[1,256,256]{2,1,0:T(8,128)(2,1)} %param.8) | copy-start | bytes 393220
  12.4 14.5 %copy-start.5 = (s32[1,256,1]{1,2,0:T(1,128)S(1)}, s32[1,256,1]{1,2,0:T(1,128)}, u32[]{:S(2)}) copy-start(s32[1,256,1]{1,2,0:T(1,128)} %param.14) | copy-start | bytes 3076
  12.4 15.4 %copy-start.7 = (s32[1,256]{1,0:T(1,128)S(1)}, s32[1,256]{1,0:T(1,128)}, u32[]{:S(2)}) copy-start(s32[1,256]{1,0:T(1,128)} %param.15) | copy-start | bytes 3076
  12.4 220.3 %all-to-all-start = ((bf16[64,256,256]{2,1,0:T(8,128)(2,1)}), bf16[64,256,256]{2,1,0:T(8,128)(2,1)}, u32[]{:S(2)}, u32[]{:S(2)}) async-start(bf16[64,256,256]{2,1,0:T(8,128)(2,1)} %stack.3), calls=%async_computation | async-start | bytes 16777216 | tf_op jit(solution)/shard_map/all_to_all | solution.py:14
  25.7 334.9 %all-gather.2.cloned.1.call-start = ((), (), s32[]{:S(2)}) async-start(), calls=%async_computation.7 | async-start | bytes 8519680 | tf_op jit(solution)/shard_map/all_gather | solution.py:139
  244.2 8.2 %copy-start.6 = (f32[1,256]{1,0:T(1,128)S(1)}, f32[1,256]{1,0:T(1,128)}, u32[]{:S(2)}) copy-start(f32[1,256]{1,0:T(1,128)} %param.12) | copy-start | bytes 3076
  244.2 8.2 %copy-start.8 = (s32[1,256]{1,0:T(1,128)S(1)}, s32[1,256]{1,0:T(1,128)}, u32[]{:S(2)}) copy-start(s32[1,256]{1,0:T(1,128)} %param.13) | copy-start | bytes 3076
  265.3 95.2 %copy-start.2 = (bf16[1,256,256]{2,1,0:T(8,128)(2,1)S(1)}, bf16[1,256,256]{2,1,0:T(8,128)(2,1)}, u32[]{:S(2)}) copy-start(bf16[1,256,256]{2,1,0:T(8,128)(2,1)} %param.11) | copy-start | bytes 393220
  267.6 17.9 %all-to-all-start.1 = ((f32[8,32,512]{2,1,0:T(8,128)}), f32[8,32,512]{2,1,0:T(8,128)S(1)}, u32[]{:S(2)}, u32[]{:S(2)}) async-start(f32[8,32,512]{2,1,0:T(8,128)} %copy.25), calls=%async_computation.1 | async-start | bytes 1048576 | tf_op jit(solution)/shard_map/all_to_all | solution.py:38
  286.2 50.8 %all-to-all-start.2 = ((f32[32,1,512]{2,1,0:T(1,128)}), f32[32,1,512]{2,1,0:T(1,128)S(1)}, u32[]{:S(2)}, u32[]{:S(2)}) async-start(f32[32,1,512]{2,1,0:T(1,128)} %all_to_all.27), calls=%async_computation.2 | async-start | bytes 131072 | tf_op jit(solution)/shard_map/all_to_all | solution.py:46
  337.7 15.6 %all-to-all-start.3 = ((f32[32,1,512]{2,1,0:T(1,128)}), f32[32,1,512]{2,1,0:T(1,128)S(1)}, u32[]{:S(2)}, u32[]{:S(2)}) async-start(f32[32,1,512]{2,1,0:T(1,128)} %broadcast_in_dim.17), calls=%async_computation.3 | async-start | bytes 131072 | tf_op jit(solution)/shard_map/all_to_all | solution.py:59
  354.0 19.4 %all-to-all-start.5 = ((f32[256,1,16,1]{2,3,1,0:T(1,128)}), f32[256,1,16,1]{2,3,1,0:T(1,128)S(1)}, u32[]{:S(2)}, u32[]{:S(2)}) async-start(f32[256,1,16,1]{2,3,1,0:T(1,128)} %bitcast.15), calls=%async_computation.5 | async-start | bytes 262144 | tf_op jit(solution)/shard_map/all_to_all | solution.py:97
  374.3 21.8 %all-to-all-start.4 = ((f32[8,32,512]{2,1,0:T(8,128)}), f32[8,32,512]{2,1,0:T(8,128)}, u32[]{:S(2)}, u32[]{:S(2)}) async-start(f32[8,32,512]{2,1,0:T(8,128)} %broadcast_in_dim.19), calls=%async_computation.4 | async-start | bytes 1048576 | tf_op jit(solution)/shard_map/all_to_all | solution.py:59
  392.6 76.9 %copy-start.1 = (bf16[256,256]{1,0:T(8,128)(2,1)S(1)}, bf16[256,256]{1,0:T(8,128)(2,1)}, u32[]{:S(2)}) copy-start(bf16[256,256]{1,0:T(8,128)(2,1)} %param.10) | copy-start | bytes 393220
  396.1 43.2 %all-to-all-start.6 = ((f32[256,1,1024]{2,1,0:T(1,128)}), f32[256,1,1024]{2,1,0:T(1,128)S(1)}, u32[]{:S(2)}, u32[]{:S(2)}) async-start(f32[256,1,1024]{2,1,0:T(1,128)} %reshape.207), calls=%async_computation.6 | async-start | bytes 2097152 | tf_op jit(solution)/shard_map/all_to_all | solution.py:97
Sparse Core Ops, SparseCore 0:
  29.8 144.0 all-gather.1
